TPU v7x, 32 devices: a whole 2x2x4 slice. The times are simulated.
32 devices in a mesh: member: 1, span: 32 (over z, y, x, core).
Axes of the slice: x: 2, y: 2, z: 4, core: 2. Of those that a mesh axis runs over, the one named last changes fastest.
Arguments:
- field: float32 [1024, 23040], P(('member', 'span')), may hold values from -60 to 60
- day_table: int32 [1024], P('member'), may hold values from 0 to 364
- band_owner: int32 [32], P('member'), may hold values from 0 to 31, as said below
- sea_mask: int32 [23040], replicated, may hold values 0 or 1
Outputs:
- coeff_out: float32 [13, 23040], P(None, ('member', 'span'))
- variance_out: float32 [23040], P(('member', 'span'))
Inputs may be any that keep to these rules, and one draw needn't show every extreme that they name: `band_owner`: a permutation of 0 to 31.
All inputs are finite; a program needn't handle non-finite values.
Results may differ from a plain program's by a relative error of at most 0.00013.
Values sent between devices are 32-bit elements; how exact they have to be, the bound alone decides.
A program may use at most 64 MiB of HBM per device.

v0:
```python
import math

import jax
import jax.numpy as jnp
from jax import lax
from jax.sharding import PartitionSpec as P

HARMS = 6


def harmonic_basis(day_values):
    angles = day_values.astype(jnp.float32) * (2.0 * math.pi / 365.0)
    basis_rows = [jnp.ones_like(angles)]
    for order in range(1, HARMS + 1):
        basis_rows.append(jnp.cos(order * angles))
        basis_rows.append(jnp.sin(order * angles))
    return jnp.stack(basis_rows, 0)


def on_device(field, day_table, band_owner, sea_mask):
    groups = lax.axis_size("span")
    own_index = lax.axis_index("span")
    steps_dev, cells = field.shape
    band_cells = cells // groups
    design = harmonic_basis(day_table)
    total_steps = design.shape[1]
    gram_matrix = jnp.dot(design, design.T, precision=lax.Precision.HIGHEST)
    factor = jnp.linalg.cholesky(gram_matrix)
    slots = jnp.arange(groups, dtype=jnp.int32)
    own_band = jnp.sum(jnp.where(band_owner == own_index, slots, 0))
    source_band = jnp.sum(
        jnp.where(band_owner[None, :] == slots[:, None], slots[None, :], 0), axis=1
    )
    blocks = field.reshape(steps_dev, groups, band_cells)
    outgoing = jnp.take(blocks, source_band, axis=1).reshape(steps_dev, cells)
    weight_mask = lax.dynamic_slice_in_dim(sea_mask, own_band * band_cells, band_cells).astype(
        jnp.float32
    )
    series = lax.all_to_all(outgoing, "span", split_axis=1, concat_axis=0, tiled=True)
    projection = jnp.dot(design, series, precision=lax.Precision.HIGHEST)
    coeffs = jax.scipy.linalg.cho_solve((factor, True), projection)
    residual = series - jnp.dot(design.T, coeffs, precision=lax.Precision.HIGHEST)
    variance = jnp.sum(residual * residual, axis=0) / total_steps
    coeffs = coeffs * weight_mask[None, :]
    variance = variance * weight_mask
    return (coeffs, variance)


def solution(mesh):
    in_specs = (P(("member", "span"), None), P("member"), P("member"), P())
    out_specs = (P(None, ("member", "span")), P(("member", "span")))
    return jax.shard_map(
        on_device, mesh=mesh, in_specs=in_specs, out_specs=out_specs, check_vma=False
    )
```

profile of v0, /device:TPU:0, one launch (start us, length us, event | category | flops | bytes accessed | tf_op | source)
XLA Modules:
  0.0 103.2 jit_solution(3279304344381537644)
XLA Ops:
  0.6 0.8 select_reduce_fusion
  1.4 4.1 %reshape.51 = f32[32,32,720]{2,1,0:T(8,128)S(1)} reshape(f32[32,23040]{1,0:T(8,128)} %param.4) | data formatting | bytes 5898240 | tf_op jit(solution)/shard_map/reshape | solution.py:34
  5.6 3.5 %copy.13 = f32[32,32,720]{2,0,1:T(8,128)} copy(f32[32,32,720]{2,1,0:T(8,128)S(1)} %reshape.51) | data formatting | bytes 5898240 | tf_op jit(solution)/shard_map/reshape | solution.py:34
  9.1 2.6 %gather_fusion = f32[32,32,720]{2,1,0:T(8,128)S(1)} fusion(f32[32,32,720]{2,0,1:T(8,128)} %copy.13, s32[1024]{0:T(1024)S(1)} %pad_clamp_fusion), kind=kCustom, calls=%fused_computation | custom fusion | bytes 5898368 | tf_op jit(solution)/shard_map/jit(_take)/gather | solution.py:35
  11.7 2.0 %select_bitcast_fusion = f32[32,32,720]{2,0,1:T(8,128)} fusion(f32[32,32,720]{2,1,0:T(8,128)S(1)} %gather_fusion, pred[32]{0:T(512)(128)(4,1)S(1)} %compare_and_fusion), kind=kLoop, calls=%fused_computation.1 | loop fusion | flops 737280 | bytes 5898272 | tf_op jit(solution)/shard_map/jit(_take)/select_n | solution.py:35
  13.8 0.0 copy-start
  13.8 0.0 copy-start.1
  13.8 7.3 %all-to-all-start = ((f32[32,32,720]{2,0,1:T(8,128)}), f32[32,32,720]{2,0,1:T(8,128)S(1)}, u32[]{:S(2)}, u32[]{:S(2)}) async-start(f32[32,32,720]{2,0,1:T(8,128)} %select_bitcast_fusion), calls=%async_computation | async-start | bytes 6291456 | tf_op jit(solution)/shard_map/all_to_all | solution.py:39
  21.1 0.0 copy-done
  21.1 0.1 fusion.16
  21.2 0.1 stack.51
  21.3 0.2 fusion.20
  21.5 0.1 copy.12
  21.6 1.2 %cholesky.16 = f32[13,13]{1,0:T(8,128)S(1)} custom-call(f32[13,13]{1,0:T(8,128)S(1)} %fusion.5), custom_call_target="Cholesky" | custom-call | tf_op jit(solution)/shard_map/jit(cholesky)/cholesky | solution.py:28
  22.9 0.6 compare_reduce_fusion
  23.5 0.6 fusion
  24.2 1.0 custom-call.10
  25.2 0.0 copy-done.1
  25.2 0.6 fusion.18
  26.5 66.0 %all-to-all-done = f32[32,32,720]{2,0,1:T(8,128)S(1)} async-done(((f32[32,32,720]{2,0,1:T(8,128)}), f32[32,32,720]{2,0,1:T(8,128)S(1)}, u32[]{:S(2)}, u32[]{:S(2)}) %all-to-all-start) | async-done | bytes 2949152 | tf_op jit(solution)/shard_map/all_to_all | solution.py:39
  92.4 1.6 %fusion.21 = f32[13,720]{1,0:T(8,128)S(1)} fusion(f32[13,1024]{1,0:T(8,128)S(1)} %stack.51, f32[1024,720]{1,0:T(8,128)S(1)} %bitcast.40), kind=kOutput, calls=%fused_computation.46 | convolution fusion | flops 115015680 | bytes 3039808 | tf_op jit(solution)/shard_map/dot_general | solution.py:40
  94.0 2.3 %copy.14 = f32[1024,720]{0,1:T(8,128)} copy(f32[1024,720]{1,0:T(8,128)S(1)} %bitcast.41) | data formatting | bytes 5898240 | tf_op jit(solution)/shard_map/all_to_all | solution.py:39
  96.3 0.2 fusion.3
  96.6 0.2 fusion.1
  96.7 4.5 %multiply_reduce_fusion = f32[720]{0:T(1024)S(1)} fusion(f32[1024,720]{0,1:T(8,128)} %copy.14, f32[13,1024]{1,0:T(8,128)S(1)} %stack.51, f32[13,720]{1,0:T(8,128)S(1)} %fusion.1), kind=kOutput, calls=%fused_computation.2 | convolution fusion | flops 117226800 | bytes 3042688 | tf_op jit(solution)/shard_map/dot_general | solution.py:42
  101.2 1.4 %multiply_multiply_fusion = (f32[720]{0:T(1024)}, f32[720]{0:T(1024)S(1)}) fusion(f32[720]{0:T(1024)S(1)} %multiply_reduce_fusion, s32[23040]{0:T(1024)} %param.7, s32[]{:T(128)S(6)} %select_n.43), kind=kLoop, calls=%fused_computation.18 | loop fusion | flops 2160 | bytes 11524 | tf_op jit(solution)/shard_map/mul | solution.py:45
  102.6 0.6 broadcast_multiply_fusion
  (6 shorter events, 0.1 us)
Async XLA Ops:
  13.8 7.3 %copy-start = (s32[1024]{0:T(1024)S(1)}, s32[1024]{0:T(1024)}, u32[]{:S(2)}) copy-start(s32[1024]{0:T(1024)} %param.5) | copy-start | bytes 12292
  13.8 11.4 %copy-start.1 = (s32[32]{0:T(128)S(1)}, s32[32]{0:T(128)}, u32[]{:S(2)}) copy-start(s32[32]{0:T(128)} %param.6) | copy-start | bytes 388
  13.8 78.7 %all-to-all-start = ((f32[32,32,720]{2,0,1:T(8,128)}), f32[32,32,720]{2,0,1:T(8,128)S(1)}, u32[]{:S(2)}, u32[]{:S(2)}) async-start(f32[32,32,720]{2,0,1:T(8,128)} %select_bitcast_fusion), calls=%async_computation | async-start | bytes 6291456 | tf_op jit(solution)/shard_map/all_to_all | solution.py:39
where the time goes:
time: 104 us; the launch traced here: 103 us
  waiting for transfers between devices  66 us (63%)
  local copies, waits for them, and re-layouts  12.8 us (12%)
  other arithmetic  9.1 us (9%)
  starting transfers between devices  7.33 us (7%)
  matrix products  6.68 us (6%)
  between operations  1.39 us (1%)
    all_to_all x1, waiting for transfers between devices, on_device(): lax.all_to_all(outgoing, 'span', split_axis=1, concat_axis=0, tiled=True)  66 us
    reshape x2, local copies, waits for them, and re-layouts, on_device(): blocks = field.reshape(steps_dev, groups, band_cells)  7.63 us
    all_to_all x1, starting transfers between devices, on_device(): lax.all_to_all(outgoing, 'span', split_axis=1, concat_axis=0, tiled=True)  7.33 us
    dot_general x1, matrix products, on_device(): jnp.dot(design.T, coeffs, precision=lax.Precision.HIGHEST)  4.5 us
    gather x1, local copies, waits for them, and re-layouts, on_device(): outgoing = jnp.take(blocks, source_band, axis=1).reshape(steps_dev, cells)  2.64 us
    all_to_all x1, local copies, waits for them, and re-layouts, on_device(): lax.all_to_all(outgoing, 'span', split_axis=1, concat_axis=0, tiled=True)  2.3 us
  transfers between devices with their start and end apart: 1, of which 1 were waited for; matrix products, arithmetic and copies ran while one was open for 5% of the time, Pallas kernels for 0%

commit v1 on v0

v1 whole, which is shorter than its diff:
```python
import math

import jax
import jax.numpy as jnp
import numpy as np
from jax import lax
from jax.experimental import pallas as pl
from jax.experimental.pallas import tpu as pltpu
from jax.sharding import PartitionSpec as P

HARMS = 6
ROWS = 16
SUM_ROW, SQ_ROW, MASK_ROW = 0, 8, 15
COEFF_ROWS = [0] + [row for k in range(1, HARMS + 1) for row in (k, 8 + k)]
HIGH = lax.Precision.HIGHEST


def stage_orders(groups):
    bits = [1 << k for k in range(1, groups.bit_length() - 1)]
    head, tail = bits[:3], bits[3:]
    return [[1] + head[c:] + head[:c] + tail for c in range(3)]


def relative_slots(groups, order):
    slots = []
    for pos in range(groups):
        slots.append(sum(bit for k, bit in enumerate(order) if pos & (groups >> (k + 1))))
    return slots


def harmonic_rows(angles):
    width = angles.shape[1]
    order = lax.broadcasted_iota(jnp.int32, (8, width), 0)
    turned = order.astype(jnp.float32) * angles
    used = order <= HARMS
    cosines = jnp.where(used, jnp.cos(turned), 0.0)
    sines = jnp.where(used, jnp.sin(turned), 0.0)
    return jnp.concatenate([cosines, sines], axis=0)


def split3(x):
    hi = x.astype(jnp.bfloat16)
    rest = x - hi.astype(jnp.float32)
    mid = rest.astype(jnp.bfloat16)
    lo = (rest - mid.astype(jnp.float32)).astype(jnp.bfloat16)
    return hi, mid, lo


def make_kernel(groups, steps_dev, cells):
    band = cells // groups
    total_steps = groups * steps_dev
    lanes = -(-band // 128) * 128
    tiles = lanes // 128
    cuts = [128 * ((tiles * c) // 3) for c in range(4)]
    orders = stage_orders(groups)
    n_stages = len(orders[0])
    period = 128 // math.gcd(band, 128)
    period = min(period, groups)
    parts = groups // period
    part_cells = period * band

    def kernel(field_ref, day_ref, mask_ref, table_ref, coeff_ref, var_ref, *scratch):
        fld, design_ref, stat, keep = scratch[:4]
        acc = scratch[4:7]
        recv = [scratch[7 + c * n_stages : 7 + (c + 1) * n_stages] for c in range(3)]
        field_sem, send_sem, recv_sem = scratch[7 + 3 * n_stages :]
        me = lax.axis_index("span")

        def partner(bit):
            return me + bit * (1 - 2 * ((me // bit) % 2))

        barrier = pltpu.get_barrier_semaphore()
        for bit in orders[0]:
            pl.semaphore_signal(
                barrier, inc=1, device_id={"span": partner(bit)},
                device_id_type=pl.DeviceIdType.MESH,
            )
        loads = []
        for g in range(parts):
            cols = pl.ds(g * part_cells, part_cells)
            load = pltpu.make_async_copy(field_ref.at[:, cols], fld.at[:, cols], field_sem.at[g])
            load.start()
            loads.append(load)

        angles = day_ref[...].astype(jnp.float32) * (2.0 * math.pi / 365.0)
        design = harmonic_rows(angles)
        design_ref[...] = design
        first = me * steps_dev
        near = design_ref[:, pl.ds(pl.multiple_of((first // 128) * 128, 128), 128)]
        near = pltpu.roll(near, (128 - first % 128) % 128, 1)[:, :steps_dev]
        row16 = lax.broadcasted_iota(jnp.int32, (ROWS, steps_dev), 0)
        own = jnp.where(row16 == SUM_ROW, 0.0, near)
        d_hi, d_mid, d_lo = (p.astype(jnp.float32) for p in split3(own))
        none = jnp.zeros_like(d_hi)
        lhs = jnp.concatenate(
            [
                jnp.concatenate([d_hi, d_hi, d_hi], axis=1),
                jnp.concatenate([d_mid, d_mid, none], axis=1),
                jnp.concatenate([d_lo, none, none], axis=1),
            ],
            axis=0,
        ).astype(jnp.bfloat16)

        def part_stats(g, _):
            base = g * part_cells
            for j in range(period):
                off = j * band
                start = off // 128 * 128
                shift = off - start
                width = -(-(shift + band) // 128) * 128
                cols = pl.ds(pl.multiple_of(base + start, 128), width)
                values = fld[:, cols]
                total = jnp.sum(values, axis=0, keepdims=True)
                centred = values - total * (1.0 / steps_dev)
                squares = jnp.sum(centred * centred, axis=0, keepdims=True)
                rhs = jnp.concatenate(split3(centred), axis=0)
                prod = jnp.dot(lhs, rhs, preferred_element_type=jnp.float32)
                block = prod[:ROWS] + (prod[ROWS : 2 * ROWS] + prod[2 * ROWS :])
                row = lax.broadcasted_iota(jnp.int32, block.shape, 0)
                sea = mask_ref[:, cols].astype(jnp.float32)
                block = jnp.where(row == SUM_ROW, total, block)
                block = jnp.where(row == SQ_ROW, squares, block)
                block = jnp.where(row == MASK_ROW, sea, block)
                if shift:
                    block = pltpu.roll(block, width - shift, 1)
                stat[g * period + j] = block[:, :lanes]
            return 0

        for load in loads:
            load.wait()
        lax.fori_loop(0, parts, part_stats, 0)

        half = groups // 2

        def gather(c):
            def body(i, _):
                acc[c][i] = stat[table_ref[c, i], :, cuts[c] : cuts[c + 1]]
                return 0

            return body

        for c in range(3):
            lax.fori_loop(half, groups, gather(c), 0)
        pl.semaphore_wait(barrier, n_stages)

        def exchange(c, k):
            count = groups >> (k + 1)
            return pltpu.make_async_remote_copy(
                src_ref=acc[c].at[pl.ds(count, count)],
                dst_ref=recv[c][k],
                send_sem=send_sem.at[c, k],
                recv_sem=recv_sem.at[c, k],
                device_id={"span": partner(orders[c][k])},
                device_id_type=pl.DeviceIdType.MESH,
            )

        copies = [[exchange(c, k) for k in range(n_stages)] for c in range(3)]
        for c in range(3):
            copies[c][0].start()
        for c in range(3):
            lax.fori_loop(0, half, gather(c), 0)
        keep[...] = stat[table_ref[0, 0], 8:16, :]

        n_cols = 3 * n_stages
        pad_cols = -(-n_cols // 8) * 8
        step = lax.broadcasted_iota(jnp.int32, (1, total_steps), 1)
        distance = jnp.bitwise_xor(step // steps_dev, me)
        weights = []
        for c in range(3):
            seen = 0
            for k in range(n_stages):
                bit = orders[c][k]
                inside = jnp.bitwise_and(distance, groups - 1 - (seen | bit)) == 0
                sign = jnp.where(jnp.bitwise_and(distance, bit) != 0, 1.0, -1.0)
                weights.append(jnp.where(inside, sign, 0.0))
                seen |= bit
        weights += [jnp.zeros((1, total_steps), jnp.float32)] * (pad_cols - n_cols)
        weights = jnp.concatenate(weights, axis=0)
        nt = (((1,), (1,)), ((), ()))
        gram = lax.dot_general(design, design, nt, precision=HIGH, preferred_element_type=jnp.float32)
        shifts = lax.dot_general(design, weights, nt, precision=HIGH, preferred_element_type=jnp.float32)
        r_id = lax.broadcasted_iota(jnp.int32, (ROWS, ROWS), 0)
        c_id = lax.broadcasted_iota(jnp.int32, (ROWS, ROWS), 1)
        eye = (r_id == c_id).astype(jnp.float32)
        unused = (r_id == HARMS + 1) | (r_id == SQ_ROW) | (r_id == MASK_ROW)
        left = jnp.where(unused, eye, gram)
        right = eye
        for k in COEFF_ROWS:
            scale = 1.0 / left[k : k + 1, k : k + 1]
            l_row = left[k : k + 1, :] * scale
            r_row = right[k : k + 1, :] * scale
            column = left[:, k : k + 1]
            left = jnp.where(r_id == k, l_row, left - column * l_row)
            right = jnp.where(r_id == k, r_row, right - column * r_row)
        inverse = right

        row1 = lax.broadcasted_iota(jnp.int32, (ROWS, 1), 0)
        plain = (row1 == SUM_ROW) | (row1 == SQ_ROW) | (row1 == MASK_ROW)

        def merge(c, k):
            n = float(steps_dev << k)
            q = c * n_stages + k
            slope = jnp.where(plain, 0.0, shifts[:, q : q + 1])
            bend = jnp.where(row1 == SQ_ROW, 2.0 * n, 0.0)

            def body(i, _):
                mine, theirs = acc[c][i], recv[c][k][i]
                gap = (theirs[SUM_ROW : SUM_ROW + 1] - mine[SUM_ROW : SUM_ROW + 1]) * (0.5 / n)
                acc[c][i] = (mine + theirs) + gap * (slope + bend * gap)
                return 0

            return body

        for k in range(n_stages):
            count = groups >> (k + 1)
            for c in range(3):
                copies[c][k].wait_recv()
                if count > 1:
                    lax.fori_loop(count // 2, count, merge(c, k), 0)
                    lax.fori_loop(0, count // 2, merge(c, k), 0)
                    copies[c][k + 1].start()
                else:
                    merge(c, k)(0, 0)

        for c in range(3):
            lo, hi = cuts[c], min(cuts[c + 1], band)
            block = acc[c][0][:, : hi - lo]
            sea = keep[MASK_ROW - 8 : MASK_ROW - 7, lo:hi]
            mean = block[SUM_ROW : SUM_ROW + 1] * (1.0 / total_steps)
            moments = jnp.where(plain, 0.0, block)
            fit = jnp.dot(inverse, moments, precision=HIGH, preferred_element_type=jnp.float32)
            explained = jnp.sum(fit * moments, axis=0, keepdims=True)
            var = (block[SQ_ROW : SQ_ROW + 1] - explained) * (1.0 / total_steps)
            var_ref[:, lo:hi] = var * sea
            fit = jnp.where(row1 == SUM_ROW, fit + mean, fit) * sea
            for j, row in enumerate(COEFF_ROWS):
                coeff_ref[j : j + 1, lo:hi] = fit[row : row + 1]
        for c in range(3):
            for k in range(n_stages):
                copies[c][k].wait_send()

    scratch = [
        pltpu.VMEM((steps_dev, cells), jnp.float32),
        pltpu.VMEM((ROWS, total_steps), jnp.float32),
        pltpu.VMEM((groups, ROWS, lanes), jnp.float32),
        pltpu.VMEM((8, lanes), jnp.float32),
    ]
    for c in range(3):
        scratch.append(pltpu.VMEM((groups, ROWS, cuts[c + 1] - cuts[c]), jnp.float32))
    for c in range(3):
        for k in range(n_stages):
            scratch.append(
                pltpu.VMEM((groups >> (k + 1), ROWS, cuts[c + 1] - cuts[c]), jnp.float32)
            )
    scratch += [
        pltpu.SemaphoreType.DMA((parts,)),
        pltpu.SemaphoreType.DMA((3, n_stages)),
        pltpu.SemaphoreType.DMA((3, n_stages)),
    ]
    vmem = pl.BlockSpec(memory_space=pltpu.VMEM)
    return pl.pallas_call(
        kernel,
        name="harmonic_fit",
        out_shape=(
            jax.ShapeDtypeStruct((2 * HARMS + 1, band), jnp.float32),
            jax.ShapeDtypeStruct((1, band), jnp.float32),
        ),
        in_specs=[
            pl.BlockSpec(memory_space=pl.ANY), vmem, vmem,
            pl.BlockSpec(memory_space=pltpu.SMEM),
        ],
        out_specs=(vmem, vmem),
        scratch_shapes=scratch,
        compiler_params=pltpu.CompilerParams(
            collective_id=0, has_side_effects=True, vmem_limit_bytes=65_000_000
        ),
    )


def on_device(field, day_table, band_owner, sea_mask):
    groups = lax.axis_size("span")
    own_index = lax.axis_index("span")
    steps_dev, cells = field.shape
    relative = np.array([relative_slots(groups, order) for order in stage_orders(groups)], np.int32)
    slots = jnp.bitwise_xor(jnp.asarray(relative), own_index)
    bands = jnp.arange(groups, dtype=jnp.int32)
    table = jnp.sum(
        jnp.where(band_owner[None, None, :] == slots[:, :, None], bands[None, None, :], 0), axis=2
    )
    coeffs, variance = make_kernel(groups, steps_dev, cells)(
        field, day_table.reshape(1, -1), sea_mask.reshape(1, -1), table
    )
    return (coeffs, variance.reshape(-1))


def solution(mesh):
    in_specs = (P(("member", "span"), None), P("member"), P("member"), P())
    out_specs = (P(None, ("member", "span")), P(("member", "span")))
    return jax.shard_map(
        on_device, mesh=mesh, in_specs=in_specs, out_specs=out_specs, check_vma=False
    )
```

time: 104 us -> 38.3 us (0.37)
  waiting for transfers between devices: 66 us -> 0 us
  Pallas kernels: 0 us -> 30.9 us
  local copies, waits for them, and re-layouts: 12.8 us -> 3 us
  starting transfers between devices: 7.33 us -> 0 us
  matrix products: 6.68 us -> 0 us
  other arithmetic: 9.1 us -> 3.43 us
    all_to_all x1 -> x0, waiting for transfers between devices: 66 us -> none  [on_device(): lax.all_to_all(outgoing, 'span', split_axis=1, concat_axis=0, tiled=True)]
    pallas_call x0 -> x1, Pallas kernels: none -> 30.9 us  [on_device(): make_kernel(groups, steps_dev, cells)]
    all_to_all x1 -> x0, starting transfers between devices: 7.33 us -> none  [on_device(): lax.all_to_all(outgoing, 'span', split_axis=1, concat_axis=0, tiled=True)]
    dot_general x3 -> x0, matrix products: 6.25 us -> none  [the longest x1 4.5 us: on_device(): jnp.dot(design.T, coeffs, precision=lax.Precision.HIGHEST)]
    reshape x2 -> x1, local copies, waits for them, and re-layouts: 7.63 us -> 1.58 us  [on_device(): sea_mask.reshape(1, -1)]
    another operation x5 -> x0, other arithmetic: 3.52 us -> none  [the longest x3 1.87 us: on_device(): factor = jnp.linalg.cholesky(gram_matrix)]
    gather x1 -> x0, local copies, waits for them, and re-layouts: 2.64 us -> none  [on_device(): outgoing = jnp.take(blocks, source_band, axis=1).reshape(steps_dev, cells)]
    all_to_all x1 -> x0, local copies, waits for them, and re-layouts: 2.3 us -> none  [on_device(): lax.all_to_all(outgoing, 'span', split_axis=1, concat_axis=0, tiled=True)]
  transfers between devices with their start and end apart: 1 -> 0, of which waited for: 1 -> 0; matrix products, arithmetic and copies ran while one was open for 5% -> 0% of each run, Pallas kernels for 0% -> 0%
where the time goes in v1:
time: 38.3 us; the launch traced here: 37.9 us
  Pallas kernels  30.9 us (81%)
  other arithmetic  3.43 us (9%)
  local copies, waits for them, and re-layouts  3 us (8%)
  between operations  0.64 us (2%)
    pallas_call x1, Pallas kernels, on_device(): make_kernel(groups, steps_dev, cells)  30.9 us
    reshape x1, local copies, waits for them, and re-layouts, on_device(): sea_mask.reshape(1, -1)  1.58 us
    reduce_sum x1, other arithmetic, on_device(): jnp.sum(jnp.where(band_owner[None, None, :] == slots[:, :, None], bands[N...  1.45 us
    unnamed x1, local copies, waits for them, and re-layouts  1.42 us
    pallas_call x1, other arithmetic, on_device(): make_kernel(groups, steps_dev, cells)  1.29 us

profile of v1, /device:TPU:0, one launch (start us, length us, event | category | flops | bytes accessed | tf_op | source)
XLA Modules:
  0.0 37.9 jit_solution(8764888046384093654)
XLA Ops:
  0.6 0.7 %broadcast_xor_fusion = s32[3,32]{1,0:T(4,128)S(1)} fusion(s32[3,32]{1,0:T(4,128)} %constant.8.clone, s32[]{:T(128)S(6)} %axis_index.12), kind=kLoop, calls=%fused_computation.1 | loop fusion | flops 96 | bytes 772 | tf_op jit(solution)/shard_map/xor | solution.py:285
  1.3 1.4 %select_reduce_fusion.table_ref = s32[3,32]{1,0:T(4,128)} fusion(s32[3,32]{1,0:T(4,128)S(1)} %broadcast_xor_fusion, s32[32]{0:T(128)} %param.7), kind=kLoop, calls=%fused_computation | loop fusion | flops 9120 | bytes 896 | tf_op jit(solution)/shard_map/reduce_sum | solution.py:287
  2.8 1.6 %reshape.16.mask_ref = s32[1,23040]{1,0:T(1,128)} reshape(s32[23040]{0:T(1024)} %param.8) | data formatting | bytes 184320 | tf_op jit(solution)/shard_map/reshape | solution.py:291
  4.3 30.9 %harmonic_fit.1 = (f32[13,720]{1,0:T(8,128)}, f32[1,720]{1,0:T(1,128)}) custom-call(f32[32,23040]{1,0:T(8,128)} %field_ref.1, s32[1,1024]{1,0:T(1,128)} %bitcast.1, s32[1,23040]{1,0:T(1,128)} %reshape.16.mask_ref, s32[3,32]{1,0:T(4,128)} %select_reduce_fusion.table_ref), custom_call_target="tpu_custom_call" | custom-call | tf_op jit(solution)/shard_map/harmonic_fit/pallas_call | solution.py:290
  35.2 1.3 %reduce = f32[720]{0:T(1024)} reduce(f32[1,720]{1,0:T(1,128)} %get-tuple-element.5, f32[]{:T(128)} %constant.9), dimensions={0}, to_apply=%get-tuple-element.5.reduce_sub_computation | reduce | bytes 5764 | tf_op jit(solution)/shard_map/harmonic_fit/pallas_call | solution.py:290
  36.5 1.4 %copy.8 = f32[13,720]{1,0:T(8,128)} copy(f32[13,720]{1,0:T(8,128)} %get-tuple-element.8) | data formatting | bytes 74880

commit v2 on v1

--- a/solution.py
+++ b/solution.py
@@ -140,25 +140,33 @@
             return body
 
         for c in range(3):
-            lax.fori_loop(half, groups, gather(c), 0)
+            lax.fori_loop(half, groups, gather(c), 0, unroll=8)
         pl.semaphore_wait(barrier, n_stages)
 
-        def exchange(c, k):
+        def exchange(c, k, part):
             count = groups >> (k + 1)
+            low, size = (count // 2, count - count // 2) if part == 0 else (0, count // 2)
             return pltpu.make_async_remote_copy(
-                src_ref=acc[c].at[pl.ds(count, count)],
-                dst_ref=recv[c][k],
-                send_sem=send_sem.at[c, k],
-                recv_sem=recv_sem.at[c, k],
+                src_ref=acc[c].at[pl.ds(count + low, size)],
+                dst_ref=recv[c][k].at[pl.ds(low, size)],
+                send_sem=send_sem.at[c, k, part],
+                recv_sem=recv_sem.at[c, k, part],
                 device_id={"span": partner(orders[c][k])},
                 device_id_type=pl.DeviceIdType.MESH,
             )
 
-        copies = [[exchange(c, k) for k in range(n_stages)] for c in range(3)]
-        for c in range(3):
-            copies[c][0].start()
-        for c in range(3):
-            lax.fori_loop(0, half, gather(c), 0)
+        copies = [
+            [
+                [exchange(c, k, part) for part in range(2 if groups >> (k + 1) > 1 else 1)]
+                for k in range(n_stages)
+            ]
+            for c in range(3)
+        ]
+        for part in range(2):
+            for c in range(3):
+                copies[c][0][part].start()
+        for c in range(3):
+            lax.fori_loop(0, half, gather(c), 0, unroll=8)
         keep[...] = stat[table_ref[0, 0], 8:16, :]
 
         n_cols = 3 * n_stages
@@ -177,23 +185,7 @@
         weights += [jnp.zeros((1, total_steps), jnp.float32)] * (pad_cols - n_cols)
         weights = jnp.concatenate(weights, axis=0)
         nt = (((1,), (1,)), ((), ()))
-        gram = lax.dot_general(design, design, nt, precision=HIGH, preferred_element_type=jnp.float32)
         shifts = lax.dot_general(design, weights, nt, precision=HIGH, preferred_element_type=jnp.float32)
-        r_id = lax.broadcasted_iota(jnp.int32, (ROWS, ROWS), 0)
-        c_id = lax.broadcasted_iota(jnp.int32, (ROWS, ROWS), 1)
-        eye = (r_id == c_id).astype(jnp.float32)
-        unused = (r_id == HARMS + 1) | (r_id == SQ_ROW) | (r_id == MASK_ROW)
-        left = jnp.where(unused, eye, gram)
-        right = eye
-        for k in COEFF_ROWS:
-            scale = 1.0 / left[k : k + 1, k : k + 1]
-            l_row = left[k : k + 1, :] * scale
-            r_row = right[k : k + 1, :] * scale
-            column = left[:, k : k + 1]
-            left = jnp.where(r_id == k, l_row, left - column * l_row)
-            right = jnp.where(r_id == k, r_row, right - column * r_row)
-        inverse = right
-
         row1 = lax.broadcasted_iota(jnp.int32, (ROWS, 1), 0)
         plain = (row1 == SUM_ROW) | (row1 == SQ_ROW) | (row1 == MASK_ROW)
 
@@ -211,16 +203,41 @@
 
             return body
 
+        def invert_gram():
+            gram = lax.dot_general(
+                design, design, nt, precision=HIGH, preferred_element_type=jnp.float32
+            )
+            r_id = lax.broadcasted_iota(jnp.int32, (ROWS, ROWS), 0)
+            c_id = lax.broadcasted_iota(jnp.int32, (ROWS, ROWS), 1)
+            eye = (r_id == c_id).astype(jnp.float32)
+            unused = (r_id == HARMS + 1) | (r_id == SQ_ROW) | (r_id == MASK_ROW)
+            left = jnp.where(unused, eye, gram)
+            right = eye
+            for k in COEFF_ROWS:
+                scale = 1.0 / left[k : k + 1, k : k + 1]
+                l_row = left[k : k + 1, :] * scale
+                r_row = right[k : k + 1, :] * scale
+                column = left[:, k : k + 1]
+                left = jnp.where(r_id == k, l_row, left - column * l_row)
+                right = jnp.where(r_id == k, r_row, right - column * r_row)
+            return right
+
         for k in range(n_stages):
             count = groups >> (k + 1)
             for c in range(3):
-                copies[c][k].wait_recv()
+                copies[c][k][0].wait_recv()
+                for i in reversed(range(count // 2, count)):
+                    merge(c, k)(i, 0)
                 if count > 1:
-                    lax.fori_loop(count // 2, count, merge(c, k), 0)
-                    lax.fori_loop(0, count // 2, merge(c, k), 0)
-                    copies[c][k + 1].start()
-                else:
-                    merge(c, k)(0, 0)
+                    for copy in copies[c][k + 1]:
+                        copy.start()
+            if k == 0:
+                inverse = invert_gram()
+            if count > 1:
+                for c in range(3):
+                    copies[c][k][1].wait_recv()
+                    for i in range(count // 2):
+                        merge(c, k)(i, 0)
 
         for c in range(3):
             lo, hi = cuts[c], min(cuts[c + 1], band)
@@ -237,7 +254,8 @@
                 coeff_ref[j : j + 1, lo:hi] = fit[row : row + 1]
         for c in range(3):
             for k in range(n_stages):
-                copies[c][k].wait_send()
+                for copy in copies[c][k]:
+                    copy.wait_send()
 
     scratch = [
         pltpu.VMEM((steps_dev, cells), jnp.float32),
@@ -254,8 +272,8 @@
             )
     scratch += [
         pltpu.SemaphoreType.DMA((parts,)),
-        pltpu.SemaphoreType.DMA((3, n_stages)),
-        pltpu.SemaphoreType.DMA((3, n_stages)),
+        pltpu.SemaphoreType.DMA((3, n_stages, 2)),
+        pltpu.SemaphoreType.DMA((3, n_stages, 2)),
     ]
     vmem = pl.BlockSpec(memory_space=pltpu.VMEM)
     return pl.pallas_call(

time: 38.3 us -> 33.7 us (0.88)
  Pallas kernels: 30.9 us -> 26.3 us
    pallas_call x1, Pallas kernels: 30.9 us -> 26.3 us  [on_device(): make_kernel(groups, steps_dev, cells)]
where the time goes in v2:
time: 33.7 us; the launch traced here: 33.3 us
  Pallas kernels  26.3 us (78%)
  other arithmetic  3.43 us (10%)
  local copies, waits for them, and re-layouts  3 us (9%)
  between operations  0.64 us (2%)
    pallas_call x1, Pallas kernels, on_device(): make_kernel(groups, steps_dev, cells)  26.3 us
    reshape x1, local copies, waits for them, and re-layouts, on_device(): sea_mask.reshape(1, -1)  1.58 us
    reduce_sum x1, other arithmetic, on_device(): jnp.sum(jnp.where(band_owner[None, None, :] == slots[:, :, None], bands[N...  1.45 us
    unnamed x1, local copies, waits for them, and re-layouts  1.42 us
    pallas_call x1, other arithmetic, on_device(): make_kernel(groups, steps_dev, cells)  1.29 us
    xor x1, other arithmetic, on_device(): slots = jnp.bitwise_xor(jnp.asarray(relative), own_index)  0.69 us

profile of v2, /device:TPU:0, one launch (start us, length us, event | category | flops | bytes accessed | tf_op | source)
XLA Modules:
  0.0 33.3 jit_solution(8818539346585283654)
XLA Ops:
  0.6 0.7 %broadcast_xor_fusion = s32[3,32]{1,0:T(4,128)S(1)} fusion(s32[3,32]{1,0:T(4,128)} %constant.8.clone, s32[]{:T(128)S(6)} %axis_index.12), kind=kLoop, calls=%fused_computation.1 | loop fusion | flops 96 | bytes 772 | tf_op jit(solution)/shard_map/xor | solution.py:303
  1.3 1.4 %select_reduce_fusion.table_ref = s32[3,32]{1,0:T(4,128)} fusion(s32[3,32]{1,0:T(4,128)S(1)} %broadcast_xor_fusion, s32[32]{0:T(128)} %param.7), kind=kLoop, calls=%fused_computation | loop fusion | flops 9120 | bytes 896 | tf_op jit(solution)/shard_map/reduce_sum | solution.py:305
  2.8 1.6 %reshape.16.mask_ref = s32[1,23040]{1,0:T(1,128)} reshape(s32[23040]{0:T(1024)} %param.8) | data formatting | bytes 184320 | tf_op jit(solution)/shard_map/reshape | solution.py:309
  4.3 26.3 %harmonic_fit.1 = (f32[13,720]{1,0:T(8,128)}, f32[1,720]{1,0:T(1,128)}) custom-call(f32[32,23040]{1,0:T(8,128)} %field_ref.1, s32[1,1024]{1,0:T(1,128)} %bitcast.1, s32[1,23040]{1,0:T(1,128)} %reshape.16.mask_ref, s32[3,32]{1,0:T(4,128)} %select_reduce_fusion.table_ref), custom_call_target="tpu_custom_call" | custom-call | tf_op jit(solution)/shard_map/harmonic_fit/pallas_call | solution.py:308
  30.6 1.3 %reduce = f32[720]{0:T(1024)} reduce(f32[1,720]{1,0:T(1,128)} %get-tuple-element.5, f32[]{:T(128)} %constant.9), dimensions={0}, to_apply=%get-tuple-element.5.reduce_sub_computation | reduce | bytes 5764 | tf_op jit(solution)/shard_map/harmonic_fit/pallas_call | solution.py:308
  31.9 1.4 %copy.8 = f32[13,720]{1,0:T(8,128)} copy(f32[13,720]{1,0:T(8,128)} %get-tuple-element.8) | data formatting | bytes 74880

commit v3 on v2

--- a/solution.py
+++ b/solution.py
@@ -2,7 +2,6 @@
 
 import jax
 import jax.numpy as jnp
-import numpy as np
 from jax import lax
 from jax.experimental import pallas as pl
 from jax.experimental.pallas import tpu as pltpu
@@ -59,11 +58,11 @@
     parts = groups // period
     part_cells = period * band
 
-    def kernel(field_ref, day_ref, mask_ref, table_ref, coeff_ref, var_ref, *scratch):
-        fld, design_ref, stat, keep = scratch[:4]
-        acc = scratch[4:7]
-        recv = [scratch[7 + c * n_stages : 7 + (c + 1) * n_stages] for c in range(3)]
-        field_sem, send_sem, recv_sem = scratch[7 + 3 * n_stages :]
+    def kernel(field_ref, day_ref, owner_ref, stat_out, inverse_out, *scratch):
+        fld, design_ref, stat, table_v, table_s = scratch[:5]
+        acc = scratch[5:8]
+        recv = [scratch[8 + c * n_stages : 8 + (c + 1) * n_stages] for c in range(3)]
+        field_sem, table_sem, send_sem, recv_sem = scratch[8 + 3 * n_stages :]
         me = lax.axis_index("span")
 
         def partner(bit):
@@ -81,6 +80,14 @@
             load = pltpu.make_async_copy(field_ref.at[:, cols], fld.at[:, cols], field_sem.at[g])
             load.start()
             loads.append(load)
+
+        slot = jnp.bitwise_xor(lax.broadcasted_iota(jnp.int32, (groups, groups), 0), me)
+        bands = lax.broadcasted_iota(jnp.int32, (groups, groups), 1)
+        placed = jnp.where(owner_ref[...] == slot, bands, 0)
+        held = jnp.minimum(jnp.sum(placed, axis=1, keepdims=True), groups - 1)
+        table_v[...] = jnp.broadcast_to(held, table_v.shape)
+        to_scalars = pltpu.make_async_copy(table_v, table_s, table_sem)
+        to_scalars.start()
 
         angles = day_ref[...].astype(jnp.float32) * (2.0 * math.pi / 365.0)
         design = harmonic_rows(angles)
@@ -117,10 +124,8 @@
                 prod = jnp.dot(lhs, rhs, preferred_element_type=jnp.float32)
                 block = prod[:ROWS] + (prod[ROWS : 2 * ROWS] + prod[2 * ROWS :])
                 row = lax.broadcasted_iota(jnp.int32, block.shape, 0)
-                sea = mask_ref[:, cols].astype(jnp.float32)
                 block = jnp.where(row == SUM_ROW, total, block)
                 block = jnp.where(row == SQ_ROW, squares, block)
-                block = jnp.where(row == MASK_ROW, sea, block)
                 if shift:
                     block = pltpu.roll(block, width - shift, 1)
                 stat[g * period + j] = block[:, :lanes]
@@ -132,15 +137,15 @@
 
         half = groups // 2
 
-        def gather(c):
-            def body(i, _):
-                acc[c][i] = stat[table_ref[c, i], :, cuts[c] : cuts[c + 1]]
-                return 0
-
-            return body
-
-        for c in range(3):
-            lax.fori_loop(half, groups, gather(c), 0, unroll=8)
+        slots = [relative_slots(groups, order) for order in orders]
+
+        def gather(c, i):
+            acc[c][i] = stat[table_s[slots[c][i], 0], :, cuts[c] : cuts[c + 1]]
+
+        to_scalars.wait()
+        for i in range(half, groups):
+            for c in range(3):
+                gather(c, i)
         pl.semaphore_wait(barrier, n_stages)
 
         def exchange(c, k, part):
@@ -165,9 +170,9 @@
         for part in range(2):
             for c in range(3):
                 copies[c][0][part].start()
-        for c in range(3):
-            lax.fori_loop(0, half, gather(c), 0, unroll=8)
-        keep[...] = stat[table_ref[0, 0], 8:16, :]
+        for i in range(half):
+            for c in range(3):
+                gather(c, i)
 
         n_cols = 3 * n_stages
         pad_cols = -(-n_cols // 8) * 8
@@ -232,7 +237,7 @@
                     for copy in copies[c][k + 1]:
                         copy.start()
             if k == 0:
-                inverse = invert_gram()
+                inverse_out[...] = invert_gram()
             if count > 1:
                 for c in range(3):
                     copies[c][k][1].wait_recv()
@@ -240,18 +245,7 @@
                         merge(c, k)(i, 0)
 
         for c in range(3):
-            lo, hi = cuts[c], min(cuts[c + 1], band)
-            block = acc[c][0][:, : hi - lo]
-            sea = keep[MASK_ROW - 8 : MASK_ROW - 7, lo:hi]
-            mean = block[SUM_ROW : SUM_ROW + 1] * (1.0 / total_steps)
-            moments = jnp.where(plain, 0.0, block)
-            fit = jnp.dot(inverse, moments, precision=HIGH, preferred_element_type=jnp.float32)
-            explained = jnp.sum(fit * moments, axis=0, keepdims=True)
-            var = (block[SQ_ROW : SQ_ROW + 1] - explained) * (1.0 / total_steps)
-            var_ref[:, lo:hi] = var * sea
-            fit = jnp.where(row1 == SUM_ROW, fit + mean, fit) * sea
-            for j, row in enumerate(COEFF_ROWS):
-                coeff_ref[j : j + 1, lo:hi] = fit[row : row + 1]
+            stat_out[:, cuts[c] : cuts[c + 1]] = acc[c][0]
         for c in range(3):
             for k in range(n_stages):
                 for copy in copies[c][k]:
@@ -261,7 +255,8 @@
         pltpu.VMEM((steps_dev, cells), jnp.float32),
         pltpu.VMEM((ROWS, total_steps), jnp.float32),
         pltpu.VMEM((groups, ROWS, lanes), jnp.float32),
-        pltpu.VMEM((8, lanes), jnp.float32),
+        pltpu.VMEM((groups, 128), jnp.int32),
+        pltpu.SMEM((groups, 128), jnp.int32),
     ]
     for c in range(3):
         scratch.append(pltpu.VMEM((groups, ROWS, cuts[c + 1] - cuts[c]), jnp.float32))
@@ -272,6 +267,7 @@
             )
     scratch += [
         pltpu.SemaphoreType.DMA((parts,)),
+        pltpu.SemaphoreType.DMA,
         pltpu.SemaphoreType.DMA((3, n_stages, 2)),
         pltpu.SemaphoreType.DMA((3, n_stages, 2)),
     ]
@@ -280,13 +276,10 @@
         kernel,
         name="harmonic_fit",
         out_shape=(
-            jax.ShapeDtypeStruct((2 * HARMS + 1, band), jnp.float32),
-            jax.ShapeDtypeStruct((1, band), jnp.float32),
+            jax.ShapeDtypeStruct((ROWS, lanes), jnp.float32),
+            jax.ShapeDtypeStruct((ROWS, ROWS), jnp.float32),
         ),
-        in_specs=[
-            pl.BlockSpec(memory_space=pl.ANY), vmem, vmem,
-            pl.BlockSpec(memory_space=pltpu.SMEM),
-        ],
+        in_specs=[pl.BlockSpec(memory_space=pl.ANY), vmem, vmem],
         out_specs=(vmem, vmem),
         scratch_shapes=scratch,
         compiler_params=pltpu.CompilerParams(
@@ -295,20 +288,64 @@
     )
 
 
+def make_finish(groups, total_steps, cells):
+    band = cells // groups
+    lanes = -(-band // 128) * 128
+    mask_rows = cells // 128
+    assert cells % 128 == 0 and mask_rows >= 8 and band <= 7 * 128
+
+    def kernel(stat_ref, inverse_ref, mask_ref, owner_ref, coeff_ref, var_ref):
+        me = lax.axis_index("span")
+        own = jnp.int32(0)
+        for b in range(groups):
+            own = jnp.where(owner_ref[b] == me, b, own)
+        first = own * band
+        top = first // 128
+        shift = first - top * 128
+        base = jnp.minimum(top, mask_rows - 8)
+        window = mask_ref[pl.ds(base, 8), :].astype(jnp.float32)
+        window = pltpu.roll(window, (8 - (top - base)) % 8, 0)
+        window = pltpu.roll(window, (128 - shift) % 128, 1)
+        below = pltpu.roll(window, 7, 0)
+        lane = lax.broadcasted_iota(jnp.int32, (8, 128), 1)
+        window = jnp.where(lane < 128 - shift, window, below)
+        sea = jnp.concatenate([window[i : i + 1] for i in range(lanes // 128)], axis=1)
+
+        row1 = lax.broadcasted_iota(jnp.int32, (ROWS, 1), 0)
+        plain = (row1 == SUM_ROW) | (row1 == SQ_ROW) | (row1 == MASK_ROW)
+        block = stat_ref[...]
+        mean = block[SUM_ROW : SUM_ROW + 1] * (1.0 / total_steps)
+        moments = jnp.where(plain, 0.0, block)
+        fit = jnp.dot(inverse_ref[...], moments, precision=HIGH, preferred_element_type=jnp.float32)
+        explained = jnp.sum(fit * moments, axis=0, keepdims=True)
+        var = (block[SQ_ROW : SQ_ROW + 1] - explained) * (1.0 / total_steps) * sea
+        var_ref[...] = var[0, :band]
+        fit = jnp.where(row1 == SUM_ROW, fit + mean, fit) * sea
+        for j, row in enumerate(COEFF_ROWS):
+            coeff_ref[j : j + 1, :] = fit[row : row + 1, :band]
+
+    vmem = pl.BlockSpec(memory_space=pltpu.VMEM)
+    return pl.pallas_call(
+        kernel,
+        name="finish_fit",
+        out_shape=(
+            jax.ShapeDtypeStruct((2 * HARMS + 1, band), jnp.float32),
+            jax.ShapeDtypeStruct((band,), jnp.float32),
+        ),
+        in_specs=[vmem, vmem, vmem, pl.BlockSpec(memory_space=pltpu.SMEM)],
+        out_specs=(vmem, vmem),
+    )
+
+
 def on_device(field, day_table, band_owner, sea_mask):
     groups = lax.axis_size("span")
-    own_index = lax.axis_index("span")
     steps_dev, cells = field.shape
-    relative = np.array([relative_slots(groups, order) for order in stage_orders(groups)], np.int32)
-    slots = jnp.bitwise_xor(jnp.asarray(relative), own_index)
-    bands = jnp.arange(groups, dtype=jnp.int32)
-    table = jnp.sum(
-        jnp.where(band_owner[None, None, :] == slots[:, :, None], bands[None, None, :], 0), axis=2
-    )
-    coeffs, variance = make_kernel(groups, steps_dev, cells)(
-        field, day_table.reshape(1, -1), sea_mask.reshape(1, -1), table
-    )
-    return (coeffs, variance.reshape(-1))
+    stats, inverse = make_kernel(groups, steps_dev, cells)(
+        field, day_table.reshape(1, -1), band_owner.reshape(1, -1)
+    )
+    return make_finish(groups, groups * steps_dev, cells)(
+        stats, inverse, sea_mask.reshape(-1, 128), band_owner
+    )
 
 
 def solution(mesh):

time: 33.7 us -> 28.5 us (0.85)
  other arithmetic: 3.43 us -> 0 us
  local copies, waits for them, and re-layouts: 3 us -> 0 us
  Pallas kernels: 26.3 us -> 27.7 us
    pallas_call x0 -> x1, Pallas kernels: none -> 1.78 us  [on_device(): make_finish(groups, groups * steps_dev, cells)]
    reshape x1 -> x0, local copies, waits for them, and re-layouts: 1.58 us -> none  [on_device(): sea_mask.reshape(1, -1)]
    reduce_sum x1 -> x0, other arithmetic: 1.45 us -> none  [on_device(): jnp.sum(jnp.where(band_owner[None, None, :] == slots[:, :, None], bands[N...]
    unnamed x1 -> x0, local copies, waits for them, and re-layouts: 1.42 us -> none
    pallas_call x1 -> x0, other arithmetic: 1.29 us -> none  [on_device(): make_kernel(groups, steps_dev, cells)]
    xor x1 -> x0, other arithmetic: 0.69 us -> none  [on_device(): slots = jnp.bitwise_xor(jnp.asarray(relative), own_index)]
    pallas_call x1, Pallas kernels: 26.3 us -> 25.9 us  [on_device(): make_kernel(groups, steps_dev, cells)]
where the time goes in v3:
time: 28.5 us; the launch traced here: 28.3 us
  Pallas kernels  27.7 us (97%)
  between operations  0.64 us (2%)
    pallas_call x1, Pallas kernels, on_device(): make_kernel(groups, steps_dev, cells)  25.9 us
    pallas_call x1, Pallas kernels, on_device(): make_finish(groups, groups * steps_dev, cells)  1.78 us

profile of v3, /device:TPU:0, one launch (start us, length us, event | category | flops | bytes accessed | tf_op | source)
XLA Modules:
  0.0 28.3 jit_solution(17224579609410834979)
XLA Ops:
  0.6 25.9 %harmonic_fit.1 = (f32[16,768]{1,0:T(8,128)}, f32[16,16]{1,0:T(8,128)}) custom-call(f32[32,23040]{1,0:T(8,128)} %field_ref.1, s32[1,1024]{1,0:T(1,128)} %bitcast.4, s32[1,32]{1,0:T(1,128)} %bitcast.5), custom_call_target="tpu_custom_call" | custom-call | tf_op jit(solution)/shard_map/harmonic_fit/pallas_call | solution.py:343
  26.5 1.8 %finish_fit.1 = (f32[13,720]{1,0:T(8,128)}, f32[720]{0:T(1024)}) custom-call(f32[16,768]{1,0:T(8,128)} %get-tuple-element.4.stat_ref, f32[16,16]{1,0:T(8,128)} %get-tuple-element.5.inverse_ref, s32[180,128]{1,0:T(8,128)} %bitcast.3, s32[32]{0:T(128)} %owner_ref.1), custom_call_target="tpu_custom_call" | custom-call | tf_op jit(solution)/shard_map/finish_fit/pallas_call | solution.py:346

commit v4 on v3

--- a/solution.py
+++ b/solution.py
@@ -59,10 +59,10 @@
     part_cells = period * band
 
     def kernel(field_ref, day_ref, owner_ref, stat_out, inverse_out, *scratch):
-        fld, design_ref, stat, table_v, table_s = scratch[:5]
-        acc = scratch[5:8]
-        recv = [scratch[8 + c * n_stages : 8 + (c + 1) * n_stages] for c in range(3)]
-        field_sem, table_sem, send_sem, recv_sem = scratch[8 + 3 * n_stages :]
+        fld, stat, table_v, table_s = scratch[:4]
+        acc = scratch[4:7]
+        recv = [scratch[7 + c * n_stages : 7 + (c + 1) * n_stages] for c in range(3)]
+        field_sem, table_sem, send_sem, recv_sem = scratch[7 + 3 * n_stages :]
         me = lax.axis_index("span")
 
         def partner(bit):
@@ -74,12 +74,13 @@
                 barrier, inc=1, device_id={"span": partner(bit)},
                 device_id_type=pl.DeviceIdType.MESH,
             )
-        loads = []
+
+        def load(g):
+            cols = pl.ds(pl.multiple_of(g * part_cells, 128), part_cells)
+            return pltpu.make_async_copy(field_ref.at[:, cols], fld.at[:, cols], field_sem.at[g])
+
         for g in range(parts):
-            cols = pl.ds(g * part_cells, part_cells)
-            load = pltpu.make_async_copy(field_ref.at[:, cols], fld.at[:, cols], field_sem.at[g])
-            load.start()
-            loads.append(load)
+            load(g).start()
 
         slot = jnp.bitwise_xor(lax.broadcasted_iota(jnp.int32, (groups, groups), 0), me)
         bands = lax.broadcasted_iota(jnp.int32, (groups, groups), 1)
@@ -89,11 +90,10 @@
         to_scalars = pltpu.make_async_copy(table_v, table_s, table_sem)
         to_scalars.start()
 
-        angles = day_ref[...].astype(jnp.float32) * (2.0 * math.pi / 365.0)
-        design = harmonic_rows(angles)
-        design_ref[...] = design
+        turn = 2.0 * math.pi / 365.0
         first = me * steps_dev
-        near = design_ref[:, pl.ds(pl.multiple_of((first // 128) * 128, 128), 128)]
+        near = day_ref[:, pl.ds(pl.multiple_of((first // 128) * 128, 128), 128)]
+        near = harmonic_rows(near.astype(jnp.float32) * turn)
         near = pltpu.roll(near, (128 - first % 128) % 128, 1)[:, :steps_dev]
         row16 = lax.broadcasted_iota(jnp.int32, (ROWS, steps_dev), 0)
         own = jnp.where(row16 == SUM_ROW, 0.0, near)
@@ -110,6 +110,7 @@
 
         def part_stats(g, _):
             base = g * part_cells
+            load(g).wait()
             for j in range(period):
                 off = j * band
                 start = off // 128 * 128
@@ -131,8 +132,6 @@
                 stat[g * period + j] = block[:, :lanes]
             return 0
 
-        for load in loads:
-            load.wait()
         lax.fori_loop(0, parts, part_stats, 0)
 
         half = groups // 2
@@ -143,8 +142,8 @@
             acc[c][i] = stat[table_s[slots[c][i], 0], :, cuts[c] : cuts[c + 1]]
 
         to_scalars.wait()
-        for i in range(half, groups):
-            for c in range(3):
+        for c in range(2):
+            for i in range(half, groups):
                 gather(c, i)
         pl.semaphore_wait(barrier, n_stages)
 
@@ -167,12 +166,17 @@
             ]
             for c in range(3)
         ]
+        copies[0][0][0].start()
+        for i in range(half, groups):
+            gather(2, i)
         for part in range(2):
             for c in range(3):
-                copies[c][0][part].start()
+                if c or part:
+                    copies[c][0][part].start()
         for i in range(half):
             for c in range(3):
                 gather(c, i)
+        design = harmonic_rows(day_ref[...].astype(jnp.float32) * turn)
 
         n_cols = 3 * n_stages
         pad_cols = -(-n_cols // 8) * 8
@@ -253,7 +257,6 @@
 
     scratch = [
         pltpu.VMEM((steps_dev, cells), jnp.float32),
-        pltpu.VMEM((ROWS, total_steps), jnp.float32),
         pltpu.VMEM((groups, ROWS, lanes), jnp.float32),
         pltpu.VMEM((groups, 128), jnp.int32),
         pltpu.SMEM((groups, 128), jnp.int32),

time: 28.5 us -> 27.6 us (0.968)
  Pallas kernels: 27.7 us -> 26.8 us
    pallas_call x1, Pallas kernels: 25.9 us -> 25 us  [on_device(): make_kernel(groups, steps_dev, cells)]
where the time goes in v4:
time: 27.6 us; the launch traced here: 27.4 us
  Pallas kernels  26.8 us (97%)
  between operations  0.64 us (2%)
    pallas_call x1, Pallas kernels, on_device(): make_kernel(groups, steps_dev, cells)  25 us
    pallas_call x1, Pallas kernels, on_device(): make_finish(groups, groups * steps_dev, cells)  1.78 us

profile of v4, /device:TPU:0, one launch (start us, length us, event | category | flops | bytes accessed | tf_op | source)
XLA Modules:
  0.0 27.4 jit_solution(3116405035458275219)
XLA Ops:
  0.6 25.0 %harmonic_fit.1 = (f32[16,768]{1,0:T(8,128)}, f32[16,16]{1,0:T(8,128)}) custom-call(f32[32,23040]{1,0:T(8,128)} %field_ref.1, s32[1,1024]{1,0:T(1,128)} %bitcast.4, s32[1,32]{1,0:T(1,128)} %bitcast.5), custom_call_target="tpu_custom_call" | custom-call | tf_op jit(solution)/shard_map/harmonic_fit/pallas_call | solution.py:346
  25.6 1.8 %finish_fit.1 = (f32[13,720]{1,0:T(8,128)}, f32[720]{0:T(1024)}) custom-call(f32[16,768]{1,0:T(8,128)} %get-tuple-element.4.stat_ref, f32[16,16]{1,0:T(8,128)} %get-tuple-element.5.inverse_ref, s32[180,128]{1,0:T(8,128)} %bitcast.3, s32[32]{0:T(128)} %owner_ref.1), custom_call_target="tpu_custom_call" | custom-call | tf_op jit(solution)/shard_map/finish_fit/pallas_call | solution.py:349
